TPU v7x, 32 devices: a whole 2x2x4 slice. The times are simulated.
32 devices in a mesh: sub: 32 (over z, y, x, core).
Axes of the slice: x: 2, y: 2, z: 4, core: 2. Of those that a mesh axis runs over, the one named last changes fastest.
Arguments:
- right_side: float32 [128, 128, 512], P('sub'), may hold values from -8 to 8
- sigma: float32 [128, 128, 512], P('sub'), may hold values from 0.25 to 2
- wind: float32 [128, 128, 512], P('sub'), may hold values from -0.8 to 0.8
- local_inverse: float32 [32, 512, 512], P('sub'), may hold values from -1 to 2, as said below
- basis_y: float32 [128, 32], replicated, may hold values from -0.5 to 0.5
- basis_z: float32 [512, 64], replicated, may hold values from -0.25 to 0.25
- gamma: float32 [5, 32, 64], replicated, may hold values from 0.3 to 3
Outputs:
- solution_field: float32 [128, 128, 512], P('sub')
- residual: float32 [128, 128, 512], P('sub')
Inputs may be any that keep to these rules, and one draw needn't show every extreme that they name: `local_inverse`: each block is the identity plus a perturbation whose entries lie within 2/sqrt(512) of zero; each row of the perturbation has norm about one half.
All inputs are finite; a program needn't handle non-finite values.
Results may differ from a plain program's by a relative error of at most 0.00022.
Values sent between devices are 32-bit elements; how exact they have to be, the bound alone decides.
A program may use at most 64 MiB of HBM per device.

v0:
```python
import functools

import jax
import jax.numpy as jnp
from jax import lax
from jax.experimental import pallas as pl
from jax.experimental.pallas import tpu as pltpu
from jax.sharding import PartitionSpec as P

HIGH = lax.Precision.HIGHEST
MESH = pl.DeviceIdType.MESH
PAD = 8


def split(x):
    hi = x.astype(jnp.bfloat16)
    lo = (x - hi.astype(jnp.float32)).astype(jnp.bfloat16)
    return hi, lo


def mm(a, b):
    return jnp.dot(a, b, preferred_element_type=jnp.float32)


def mt(a, b):
    return lax.dot_general(
        a, b, (((1,), (1,)), ((), ())), preferred_element_type=jnp.float32
    )


def tm(a, b):
    return lax.dot_general(
        a, b, (((0,), (0,)), ((), ())), preferred_element_type=jnp.float32
    )


def fold(x):
    part = jnp.sum(x, axis=0, keepdims=True)
    out = part[:, 0:128]
    for at in range(128, part.shape[1], 128):
        out = out + part[:, at : at + 128]
    return out


def kernel(
    n, block,
    r_hbm, sg_hbm, wd_hbm, li_hbm, by_hbm, bz_hbm, gm_hbm,
    r, u1, u2, w1, w2, coef,
    sg, wd, lf, by, bz, gm, lh, ll, by3, bz3, hs, hr,
    own, gat, tot, allb, low_s, low_r, nbr, gs, ggat,
    in_sem, sa, ra, sb, rb, se, re, sh, rh, sga, rga,
):
    layers, rows, depth = r.shape
    ky = by.shape[0]
    half = ky // 2
    kz = bz.shape[0]
    levels = gm.shape[0]
    blocks = n // block
    low_levels = block.bit_length() - 1
    me = lax.axis_index("sub")
    p = lax.rem(me, block)
    z = lax.div(me, block)
    us = (u1, u2)
    ws = (w1, w2)

    def load(i, src, dst):
        c = pltpu.make_async_copy(src, dst, in_sem.at[i])
        c.start()
        return c

    c_r = load(0, r_hbm, r)
    c_bz = load(1, bz_hbm, bz)
    c_by = load(2, by_hbm, by)
    c_l = load(3, li_hbm, lf)
    c_gm = load(4, gm_hbm, gm)

    barrier = pltpu.get_barrier_semaphore()
    in_block = [z * block + lax.rem(p + d, block) for d in range(1, block)]
    across = [lax.rem(z + d, blocks) * block + p for d in range(1, blocks)]
    first_cross = jnp.logical_and(p == 0, z > 0)
    last_cross = jnp.logical_and(p == block - 1, z < blocks - 1)

    def signal(target):
        pl.semaphore_signal(barrier, inc=1, device_id=(target,), device_id_type=MESH)

    for target in in_block + across:
        signal(target)

    @pl.when(first_cross)
    def _():
        signal(me - 1)

    @pl.when(last_cross)
    def _():
        signal(me + 1)

    zero_rows = jnp.zeros((PAD, depth), jnp.float32)
    for u in us:
        for l in range(1, layers + 1):
            u[l, 0:PAD, :] = zero_rows
            u[l, PAD + rows : PAD + rows + PAD, :] = zero_rows

    def send(src, dst, s, q, target):
        return pltpu.make_async_remote_copy(
            src_ref=src, dst_ref=dst, send_sem=s, recv_sem=q,
            device_id=(target,), device_id_type=MESH,
        )

    def project(k, field):
        summed = field[0]
        for l in range(1, layers):
            summed = summed + field[l]
        sh_, sl_ = split(summed)
        bh, bl = bz3[0:kz], bz3[2 * kz : 3 * kz]
        part = mt(sh_, bh) + mt(sl_, bh) + mt(sh_, bl)
        ph, pl_ = split(part)
        bh, bl = by3[0:ky], by3[2 * ky : 3 * ky]
        full = mm(bh, ph) + mm(bh, pl_) + mm(bl, ph)
        packed = jnp.concatenate([full[0:half], full[half:ky]], axis=1)
        own[k] = packed
        gat[k, p] = packed

    def a_copy(k, d):
        return send(own.at[k], gat.at[k, p], sa.at[k, d], ra.at[k, p], in_block[d - 1])

    def a_arrived(k, d):
        q = lax.rem(p + d, block)
        return send(own.at[k], gat.at[k, q], sa.at[k, d], ra.at[k, q], in_block[d - 1])

    def b_copy(k, d):
        return send(tot.at[k], allb.at[k, z], sb.at[k, d], rb.at[k, z], across[d - 1])

    def b_arrived(k, d):
        q = lax.rem(z + d, blocks)
        return send(tot.at[k], allb.at[k, q], sb.at[k, d], rb.at[k, q], across[d - 1])

    def down(k):
        return send(hs.at[k, 0], hr.at[k, 1], sh.at[k, 0], rh.at[k, 1], me - 1)

    def up(k):
        return send(hs.at[k, 1], hr.at[k, 0], sh.at[k, 1], rh.at[k, 0], me + 1)

    def low_down(k):
        return send(low_s.at[k, 0], low_r.at[k, 1], se.at[k, 0], re.at[k, 1], me - block)

    def low_up(k):
        return send(low_s.at[k, 1], low_r.at[k, 0], se.at[k, 1], re.at[k, 0], me + block)

    def local(x):
        xh, xl = split(x)
        return mm(xh, lh[...]) + mm(xl, lh[...]) + mm(xh, ll[...])

    def factor(level):
        g = gm[level]
        return jnp.concatenate([g[0:half], g[half:ky]], axis=1) * (
            (layers * 2 ** (level + 1)) ** -0.5
        )

    def low_part(k, q, upper):
        out = None
        for level in range(low_levels):
            width = 2 ** (level + 1)
            start = lax.div(q, width) * width
            if width == block:
                acc = tot[k]
            else:
                acc = gat[k, start]
                for j in range(1, width):
                    acc = acc + gat[k, start + j]
            term = upper[level] * acc
            out = term if out is None else out + term
        return out

    def high_part(k, zz, upper):
        out = jnp.zeros(tot.shape[1:], jnp.float32)
        for level in range(low_levels, levels):
            width = 2 ** (level + 1) // block
            start = lax.div(zz, width) * width
            acc = allb[k, start]
            for j in range(1, width):
                acc = acc + allb[k, start + j]
            out = out + upper[level] * acc
        return out

    def edges(k, field):
        first = local(field[0])
        hs[k, 0] = first

        @pl.when(me > 0)
        def _():
            down(k).start()

        us[k][1, PAD : PAD + rows, :] = first
        last = local(field[layers - 1])
        hs[k, 1] = last

        @pl.when(me < n - 1)
        def _():
            up(k).start()

        us[k][layers, PAD : PAD + rows, :] = last

    def middle(k, field):
        for l in range(1, layers - 1):
            us[k][l + 1, PAD : PAD + rows, :] = local(field[l])

    def exchange(k):
        fac = [factor(level) for level in range(levels)]
        for d in range(1, block):
            a_arrived(k, d).wait_recv()
        acc = gat[k, 0]
        for j in range(1, block):
            acc = acc + gat[k, j]
        tot[k] = acc
        allb[k, z] = acc
        for d in range(1, blocks):
            b_copy(k, d).start()

        @pl.when(jnp.logical_and(p == block - 1, z > 0))
        def _():
            low_s[k, 0] = low_part(k, 0, fac)
            low_down(k).start()

        @pl.when(jnp.logical_and(p == 0, z < blocks - 1))
        def _():
            low_s[k, 1] = low_part(k, block - 1, fac)
            low_up(k).start()

        nbr[1] = low_part(k, p, fac)

        @pl.when(p > 0)
        def _():
            nbr[0] = low_part(k, p - 1, fac)

        @pl.when(p < block - 1)
        def _():
            nbr[2] = low_part(k, p + 1, fac)

        @pl.when(jnp.logical_and(p == 0, z == 0))
        def _():
            nbr[0] = jnp.zeros(nbr.shape[1:], jnp.float32)

        @pl.when(jnp.logical_and(p == block - 1, z == blocks - 1))
        def _():
            nbr[2] = jnp.zeros(nbr.shape[1:], jnp.float32)

        for d in range(1, blocks):
            b_arrived(k, d).wait_recv()

        @pl.when(first_cross)
        def _():
            low_up(k).wait_recv()
            nbr[0] = low_r[k, 0]

        @pl.when(last_cross)
        def _():
            low_down(k).wait_recv()
            nbr[2] = low_r[k, 1]

        here = high_part(k, z, fac)
        before = high_part(k, lax.div(lax.rem(me + n - 1, n), block), fac)
        after = high_part(k, lax.div(lax.rem(me + 1, n), block), fac)
        three = []
        for c in (nbr[0] + before, nbr[1] + here, nbr[2] + after):
            three += [c[:, 0:kz], c[:, kz : 2 * kz]]
        stack = jnp.concatenate(three, axis=0)
        th, tl = split(stack)
        back = mm(jnp.concatenate([th, tl, th], axis=1), bz3[...])
        th, tl = split(back)
        spreads = []
        for j in range(3):
            piece = slice(j * ky, (j + 1) * ky)
            spreads.append(
                tm(by3[...], jnp.concatenate([th[piece], tl[piece], th[piece]], axis=0))
            )
        u = us[k]
        mine = spreads[1]
        for l in range(1, layers + 1):
            u[l, PAD : PAD + rows, :] = u[l, PAD : PAD + rows, :] + mine
        u[0, PAD : PAD + rows, :] = jnp.where(me > 0, spreads[0], 0.0)
        u[layers + 1, PAD : PAD + rows, :] = jnp.where(me < n - 1, spreads[2], 0.0)

    step = 32

    def operator(k, l):
        u = us[k]
        col = lax.broadcasted_iota(jnp.int32, (step, depth), 1)
        for y in range(0, rows, step):
            a = PAD + y
            c = u[l + 1, a : a + step, :]
            hi = u[l + 2, a : a + step, :]
            lo = u[l, a : a + step, :]
            fwd = jnp.where(col == depth - 1, 0.0, pltpu.roll(c, depth - 1, 1))
            bwd = jnp.where(col == 0, 0.0, pltpu.roll(c, 1, 1))
            beside = (
                hi + lo + u[l + 1, a + 1 : a + step + 1, :]
                + u[l + 1, a - 1 : a + step - 1, :] + fwd + bwd
            )
            ws[k][l, y : y + step, :] = (
                (6.0 + sg[l, y : y + step, :]) * c - beside
                + wd[l, y : y + step, :] * (hi - lo)
            )

    def stencil(k):
        for l in range(layers):
            operator(k, l)

    def meet(k):
        w = ws[k]

        @pl.when(me > 0)
        def _():
            up(k).wait_recv()
            w[0] = w[0] - (1.0 + wd[0]) * hr[k, 0]

        @pl.when(me < n - 1)
        def _():
            down(k).wait_recv()
            w[layers - 1] = w[layers - 1] + (wd[layers - 1] - 1.0) * hr[k, 1]

    def dots(pairs, which):
        out = []
        for a, b in pairs:
            acc = None
            for l in which:
                term = a[l] * b[l]
                acc = term if acc is None else acc + term
            out.append(fold(acc))
        return out

    def triple(src, dst):
        hi, lo = split(src[...])
        m = src.shape[0]
        dst[0:m] = hi
        dst[m : 2 * m] = hi
        dst[2 * m : 3 * m] = lo

    c_bz.wait()
    triple(bz, bz3)
    c_by.wait()
    triple(by, by3)
    c_r.wait()
    project(0, r)
    extra = jnp.where(first_cross, 1, 0) + jnp.where(last_cross, 1, 0)
    pl.semaphore_wait(barrier, block - 1 + blocks - 1 + extra)
    for d in range(1, block):
        a_copy(0, d).start()
    c_l.wait()
    c_sg = load(5, sg_hbm, sg)
    c_wd = load(6, wd_hbm, wd)
    big, small = split(lf[0])
    lh[...] = big
    ll[...] = small
    edges(0, r)
    middle(0, r)
    c_gm.wait()
    exchange(0)
    c_sg.wait()
    c_wd.wait()
    stencil(0)
    meet(0)

    project(1, w1)
    for d in range(1, block):
        a_copy(1, d).start()
    edges(1, w1)
    middle(1, w1)
    early = dots([(r, r), (r, w1), (w1, w1)], range(layers))
    exchange(1)
    stencil(1)
    pairs = [(r, w2), (w1, w2), (w2, w2)]
    inside = dots(pairs, range(1, layers - 1))
    meet(1)
    late = [i + o for i, o in zip(inside, dots(pairs, (0, layers - 1)))]
    blank = jnp.zeros((2, 128), jnp.float32)
    sums = jnp.sum(jnp.concatenate(early + late + [blank], axis=0), axis=1, keepdims=True)
    row = lax.broadcasted_iota(jnp.int32, (8, 128), 0)
    lane = lax.broadcasted_iota(jnp.int32, (8, 128), 1)
    flat = jnp.sum(jnp.where(row == lane, sums, 0.0), axis=0, keepdims=True)
    gs[...] = flat
    ggat[me] = flat

    def g_copy(d):
        return send(gs, ggat.at[me], sga.at[d], rga.at[me], lax.rem(me + d, n))

    def g_arrived(d):
        q = lax.rem(me + d, n)
        return send(gs, ggat.at[q], sga.at[d], rga.at[q], q)

    for d in range(1, n):
        g_copy(d).start()
    for d in range(1, n):
        g_arrived(d).wait_recv()
    total = jnp.sum(ggat[...], axis=0)
    g01, g11, g02, g12, g22 = (total[:, j : j + 1] for j in range(1, 6))
    ratio = g12 / g11
    c2 = (g02 - ratio * g01) / (g22 - ratio * g12)
    c1 = g01 / g11 - ratio * c2
    coef[0:1, :] = jnp.broadcast_to(c1, (1, 128))
    coef[1:2, :] = jnp.broadcast_to(c2, (1, 128))

    for k in range(2):
        for d in range(1, block):
            a_copy(k, d).wait_send()
        for d in range(1, blocks):
            b_copy(k, d).wait_send()

        @pl.when(jnp.logical_and(p == block - 1, z > 0))
        def _():
            low_down(k).wait_send()

        @pl.when(jnp.logical_and(p == 0, z < blocks - 1))
        def _():
            low_up(k).wait_send()

        @pl.when(me > 0)
        def _():
            down(k).wait_send()

        @pl.when(me < n - 1)
        def _():
            up(k).wait_send()

    for d in range(1, n):
        g_copy(d).wait_send()


def finish(r, u1, u2, w1, w2, coef, x_hbm, res_hbm, xo, ro, out_sem):
    layers, rows, depth = r.shape
    step = 32
    c1 = coef[0:1, 0:1]
    c2 = coef[1:2, 0:1]
    outs = []
    for l in range(layers):
        for y in range(0, rows, step):
            a = PAD + y
            xo[l, y : y + step, :] = (
                c1 * u1[l + 1, a : a + step, :] + c2 * u2[l + 1, a : a + step, :]
            )
        c = pltpu.make_async_copy(xo.at[l], x_hbm.at[l], out_sem.at[0, l])
        c.start()
        outs.append(c)
    for l in range(layers):
        for y in range(0, rows, step):
            ro[l, y : y + step, :] = (
                r[l, y : y + step, :]
                - c1 * w1[l, y : y + step, :] - c2 * w2[l, y : y + step, :]
            )
        c = pltpu.make_async_copy(ro.at[l], res_hbm.at[l], out_sem.at[1, l])
        c.start()
        outs.append(c)
    for c in outs:
        c.wait()


def on_device(right_side, sigma, wind, local_inverse, basis_y, basis_z, gamma):
    n = lax.axis_size("sub")
    block = min(8, n)
    blocks = n // block
    layers, rows, depth = right_side.shape
    ky = basis_y.shape[1]
    kz = basis_z.shape[1]
    levels = gamma.shape[0]
    f32 = jnp.float32
    packed = (ky // 2, 2 * kz)
    cube = pltpu.VMEM((layers, rows, depth), f32)
    padded = pltpu.VMEM((layers + 2, rows + 2 * PAD, depth), f32)
    dma = pltpu.SemaphoreType.DMA
    scratch = [
        cube, cube,
        pltpu.VMEM((1, depth, depth), f32),
        pltpu.VMEM((ky, rows), f32),
        pltpu.VMEM((kz, depth), f32),
        pltpu.VMEM(gamma.shape, f32),
        pltpu.VMEM((depth, depth), jnp.bfloat16),
        pltpu.VMEM((depth, depth), jnp.bfloat16),
        pltpu.VMEM((3 * ky, rows), jnp.bfloat16),
        pltpu.VMEM((3 * kz, depth), jnp.bfloat16),
        pltpu.VMEM((2, 2, rows, depth), f32),
        pltpu.VMEM((2, 2, rows, depth), f32),
        pltpu.VMEM((2,) + packed, f32),
        pltpu.VMEM((2, block) + packed, f32),
        pltpu.VMEM((2,) + packed, f32),
        pltpu.VMEM((2, blocks) + packed, f32),
        pltpu.VMEM((2, 2) + packed, f32),
        pltpu.VMEM((2, 2) + packed, f32),
        pltpu.VMEM((3,) + packed, f32),
        pltpu.VMEM((1, 128), f32),
        pltpu.VMEM((n, 1, 128), f32),
        dma((7,)),
        dma((2, block)), dma((2, block)),
        dma((2, blocks)), dma((2, blocks)),
        dma((2, 2)), dma((2, 2)),
        dma((2, 2)), dma((2, 2)),
        dma((n,)), dma((n,)),
    ]
    hbm = pl.BlockSpec(memory_space=pltpu.HBM)
    vmem = pl.BlockSpec(memory_space=pltpu.VMEM)
    out = jax.ShapeDtypeStruct(right_side.shape, f32)
    pieces = pl.pallas_call(
        functools.partial(kernel, n, block),
        out_shape=(cube, padded, padded, cube, cube, pltpu.VMEM((8, 128), f32)),
        in_specs=[hbm] * 7,
        out_specs=(vmem,) * 6,
        scratch_shapes=scratch,
        compiler_params=pltpu.CompilerParams(
            collective_id=0, has_side_effects=True, vmem_limit_bytes=50 * 2**20,
        ),
        name="gmres",
    )(right_side, sigma, wind, local_inverse, basis_y.T, basis_z.T, gamma)
    return pl.pallas_call(
        finish,
        out_shape=(out, out),
        in_specs=[vmem] * 6,
        out_specs=(hbm, hbm),
        scratch_shapes=[cube, cube, dma((2, layers))],
        compiler_params=pltpu.CompilerParams(vmem_limit_bytes=24 * 2**20),
        name="finish",
    )(*pieces)


def solution(mesh):
    placed = (
        P("sub", None, None),
        P("sub", None, None),
        P("sub", None, None),
        P("sub", None, None),
        P(),
        P(),
        P(),
    )
    return jax.shard_map(
        on_device,
        mesh=mesh,
        in_specs=placed,
        out_specs=(P("sub", None, None), P("sub", None, None)),
        check_vma=False,
    )
```

profile of v0, /device:TPU:0, one launch (start us, length us, event | category | flops | bytes accessed | tf_op | source)
XLA Modules:
  0.0 32.4 jit_solution(11225971055158977164)
XLA Ops:
  0.6 30.4 %gmres.1 = (f32[4,128,512]{2,1,0:T(8,128)S(1)}, f32[6,144,512]{2,1,0:T(8,128)S(1)}, f32[6,144,512]{2,1,0:T(8,128)S(1)}, f32[4,128,512]{2,1,0:T(8,128)S(1)}, f32[...) custom-call(f32[4,128,512]{2,1,0:T(8,128)} %r_hbm.1, f32[4,128,512]{2,1,0:T(8,128)} %sg_hbm.1, f32[4,128,512]{2,1,0:T(8,128)} %wd_hbm.1, ...), custom_call_target="tpu_custom_call" | custom-call | tf_op jit(solution)/shard_map/gmres/pallas_call | solution.py:500
  31.0 1.4 %finish.1 = (f32[4,128,512]{2,1,0:T(8,128)}, f32[4,128,512]{2,1,0:T(8,128)}) custom-call(f32[4,128,512]{2,1,0:T(8,128)S(1)} %get-tuple-element.8.r, f32[6,144,512]{2,1,0:T(8,128)S(1)} %get-tuple-element.9.u1, f32[6,144,512]{2,1,0:T(8,128)S(1)} %get-tuple-element.10.u2, f32[4,128,512]{2,1,0:T(8,128)S(1)} %get-tuple-element.11.w1, ...), custom_call_target="tpu_custom_call" | custom-call | tf_op jit(solution)/shard_map/finish/pallas_call | solution.py:511
where the time goes:
time: 32.6 us; the launch traced here: 32.4 us
  Pallas kernels  31.8 us (98%)
  between operations  0.64 us (2%)
    pallas_call x1, Pallas kernels, on_device(): pl.pallas_call(functools.partial(kernel, n, block), out_shape=(cube, padd...  30.4 us
    pallas_call x1, Pallas kernels, on_device(): pl.pallas_call(finish, out_shape=(out, out), in_specs=[vmem] * 6, out_spe...  1.44 us

commit v1 on v0

--- a/solution.py
+++ b/solution.py
@@ -40,6 +40,19 @@
     for at in range(128, part.shape[1], 128):
         out = out + part[:, at : at + 128]
     return out
+
+
+def flip(i, mask):
+    out, bit = i, 1
+    while bit <= mask:
+        if mask & bit:
+            out = out + bit - 2 * bit * lax.rem(lax.div(i, bit), 2)
+        bit *= 2
+    return out
+
+
+def drain(ref, sem):
+    pltpu.make_async_copy(ref, ref, sem).wait()
 
 
 def kernel(
@@ -75,7 +88,7 @@
     c_gm = load(4, gm_hbm, gm)
 
     barrier = pltpu.get_barrier_semaphore()
-    in_block = [z * block + lax.rem(p + d, block) for d in range(1, block)]
+    in_block = [z * block + flip(p, d) for d in range(block - 1, 0, -1)]
     across = [lax.rem(z + d, blocks) * block + p for d in range(1, blocks)]
     first_cross = jnp.logical_and(p == 0, z > 0)
     last_cross = jnp.logical_and(p == block - 1, z < blocks - 1)
@@ -120,19 +133,20 @@
         own[k] = packed
         gat[k, p] = packed
 
-    def a_copy(k, d):
-        return send(own.at[k], gat.at[k, p], sa.at[k, d], ra.at[k, p], in_block[d - 1])
-
-    def a_arrived(k, d):
-        q = lax.rem(p + d, block)
-        return send(own.at[k], gat.at[k, q], sa.at[k, d], ra.at[k, q], in_block[d - 1])
-
-    def b_copy(k, d):
-        return send(tot.at[k], allb.at[k, z], sb.at[k, d], rb.at[k, z], across[d - 1])
-
-    def b_arrived(k, d):
-        q = lax.rem(z + d, blocks)
-        return send(tot.at[k], allb.at[k, q], sb.at[k, d], rb.at[k, q], across[d - 1])
+    def a_send(k):
+        for target in in_block:
+            send(own.at[k], gat.at[k, p], sa.at[k], ra.at[k], target).start()
+
+    def a_wait(k, sem):
+        drain(gat.at[k, pl.ds(0, block - 1)], sem.at[k])
+
+    def b_send(k):
+        for target in across:
+            send(tot.at[k], allb.at[k, z], sb.at[k], rb.at[k], target).start()
+
+    def b_wait(k, sem):
+        if blocks > 1:
+            drain(allb.at[k, pl.ds(0, blocks - 1)], sem.at[k])
 
     def down(k):
         return send(hs.at[k, 0], hr.at[k, 1], sh.at[k, 0], rh.at[k, 1], me - 1)
@@ -206,15 +220,13 @@
 
     def exchange(k):
         fac = [factor(level) for level in range(levels)]
-        for d in range(1, block):
-            a_arrived(k, d).wait_recv()
+        a_wait(k, ra)
         acc = gat[k, 0]
         for j in range(1, block):
             acc = acc + gat[k, j]
         tot[k] = acc
         allb[k, z] = acc
-        for d in range(1, blocks):
-            b_copy(k, d).start()
+        b_send(k)
 
         @pl.when(jnp.logical_and(p == block - 1, z > 0))
         def _():
@@ -244,8 +256,7 @@
         def _():
             nbr[2] = jnp.zeros(nbr.shape[1:], jnp.float32)
 
-        for d in range(1, blocks):
-            b_arrived(k, d).wait_recv()
+        b_wait(k, rb)
 
         @pl.when(first_cross)
         def _():
@@ -343,8 +354,7 @@
     project(0, r)
     extra = jnp.where(first_cross, 1, 0) + jnp.where(last_cross, 1, 0)
     pl.semaphore_wait(barrier, block - 1 + blocks - 1 + extra)
-    for d in range(1, block):
-        a_copy(0, d).start()
+    a_send(0)
     c_l.wait()
     c_sg = load(5, sg_hbm, sg)
     c_wd = load(6, wd_hbm, wd)
@@ -361,8 +371,7 @@
     meet(0)
 
     project(1, w1)
-    for d in range(1, block):
-        a_copy(1, d).start()
+    a_send(1)
     edges(1, w1)
     middle(1, w1)
     early = dots([(r, r), (r, w1), (w1, w1)], range(layers))
@@ -380,17 +389,9 @@
     gs[...] = flat
     ggat[me] = flat
 
-    def g_copy(d):
-        return send(gs, ggat.at[me], sga.at[d], rga.at[me], lax.rem(me + d, n))
-
-    def g_arrived(d):
-        q = lax.rem(me + d, n)
-        return send(gs, ggat.at[q], sga.at[d], rga.at[q], q)
-
-    for d in range(1, n):
-        g_copy(d).start()
-    for d in range(1, n):
-        g_arrived(d).wait_recv()
+    for d in range(n - 1, 0, -1):
+        send(gs, ggat.at[me], sga, rga, flip(me, d)).start()
+    drain(ggat.at[pl.ds(0, n - 1)], rga)
     total = jnp.sum(ggat[...], axis=0)
     g01, g11, g02, g12, g22 = (total[:, j : j + 1] for j in range(1, 6))
     ratio = g12 / g11
@@ -400,10 +401,8 @@
     coef[1:2, :] = jnp.broadcast_to(c2, (1, 128))
 
     for k in range(2):
-        for d in range(1, block):
-            a_copy(k, d).wait_send()
-        for d in range(1, blocks):
-            b_copy(k, d).wait_send()
+        a_wait(k, sa)
+        b_wait(k, sb)
 
         @pl.when(jnp.logical_and(p == block - 1, z > 0))
         def _():
@@ -421,36 +420,30 @@
         def _():
             up(k).wait_send()
 
-    for d in range(1, n):
-        g_copy(d).wait_send()
-
-
-def finish(r, u1, u2, w1, w2, coef, x_hbm, res_hbm, xo, ro, out_sem):
+    drain(ggat.at[pl.ds(0, n - 1)], sga)
+
+
+def finish(r, u1, u2, w1, w2, coef, x_hbm, res_hbm, xo, ro, out_sem, res_sem):
     layers, rows, depth = r.shape
     step = 32
     c1 = coef[0:1, 0:1]
     c2 = coef[1:2, 0:1]
-    outs = []
     for l in range(layers):
         for y in range(0, rows, step):
             a = PAD + y
             xo[l, y : y + step, :] = (
                 c1 * u1[l + 1, a : a + step, :] + c2 * u2[l + 1, a : a + step, :]
             )
-        c = pltpu.make_async_copy(xo.at[l], x_hbm.at[l], out_sem.at[0, l])
-        c.start()
-        outs.append(c)
+        pltpu.make_async_copy(xo.at[l], x_hbm.at[l], out_sem).start()
     for l in range(layers):
         for y in range(0, rows, step):
             ro[l, y : y + step, :] = (
                 r[l, y : y + step, :]
                 - c1 * w1[l, y : y + step, :] - c2 * w2[l, y : y + step, :]
             )
-        c = pltpu.make_async_copy(ro.at[l], res_hbm.at[l], out_sem.at[1, l])
-        c.start()
-        outs.append(c)
-    for c in outs:
-        c.wait()
+        pltpu.make_async_copy(ro.at[l], res_hbm.at[l], res_sem).start()
+    drain(xo, out_sem)
+    drain(ro, res_sem)
 
 
 def on_device(right_side, sigma, wind, local_inverse, basis_y, basis_z, gamma):
@@ -488,11 +481,11 @@
         pltpu.VMEM((1, 128), f32),
         pltpu.VMEM((n, 1, 128), f32),
         dma((7,)),
-        dma((2, block)), dma((2, block)),
-        dma((2, blocks)), dma((2, blocks)),
+        dma((2,)), dma((2,)),
+        dma((2,)), dma((2,)),
         dma((2, 2)), dma((2, 2)),
         dma((2, 2)), dma((2, 2)),
-        dma((n,)), dma((n,)),
+        dma, dma,
     ]
     hbm = pl.BlockSpec(memory_space=pltpu.HBM)
     vmem = pl.BlockSpec(memory_space=pltpu.VMEM)
@@ -513,7 +506,7 @@
         out_shape=(out, out),
         in_specs=[vmem] * 6,
         out_specs=(hbm, hbm),
-        scratch_shapes=[cube, cube, dma((2, layers))],
+        scratch_shapes=[cube, cube, dma, dma],
         compiler_params=pltpu.CompilerParams(vmem_limit_bytes=24 * 2**20),
         name="finish",
     )(*pieces)

time: 32.6 us -> 32.7 us (level)
  no operation moved by 1% of the time
where the time goes in v1:
time: 32.7 us; the launch traced here: 32.6 us
  Pallas kernels  31.9 us (98%)
  between operations  0.64 us (2%)
    pallas_call x1, Pallas kernels, on_device(): pl.pallas_call(functools.partial(kernel, n, block), out_shape=(cube, padd...  30.5 us
    pallas_call x1, Pallas kernels, on_device(): pl.pallas_call(finish, out_shape=(out, out), in_specs=[vmem] * 6, out_spe...  1.39 us

profile of v1, /device:TPU:0, one launch (start us, length us, event | category | flops | bytes accessed | tf_op | source)
XLA Modules:
  0.0 32.6 jit_solution(17357879756772109433)
XLA Ops:
  0.6 30.5 %gmres.1 = (f32[4,128,512]{2,1,0:T(8,128)S(1)}, f32[6,144,512]{2,1,0:T(8,128)S(1)}, f32[6,144,512]{2,1,0:T(8,128)S(1)}, f32[4,128,512]{2,1,0:T(8,128)S(1)}, f32[...) custom-call(f32[4,128,512]{2,1,0:T(8,128)} %r_hbm.1, f32[4,128,512]{2,1,0:T(8,128)} %sg_hbm.1, f32[4,128,512]{2,1,0:T(8,128)} %wd_hbm.1, ...), custom_call_target="tpu_custom_call" | custom-call | tf_op jit(solution)/shard_map/gmres/pallas_call | solution.py:493
  31.2 1.4 %finish.1 = (f32[4,128,512]{2,1,0:T(8,128)}, f32[4,128,512]{2,1,0:T(8,128)}) custom-call(f32[4,128,512]{2,1,0:T(8,128)S(1)} %get-tuple-element.8.r, f32[6,144,512]{2,1,0:T(8,128)S(1)} %get-tuple-element.9.u1, f32[6,144,512]{2,1,0:T(8,128)S(1)} %get-tuple-element.10.u2, f32[4,128,512]{2,1,0:T(8,128)S(1)} %get-tuple-element.11.w1, ...), custom_call_target="tpu_custom_call" | custom-call | tf_op jit(solution)/shard_map/finish/pallas_call | solution.py:504

commit v2 on v1

v2 whole, which is shorter than its diff:
```python
import functools

import jax
import jax.numpy as jnp
from jax import lax
from jax.experimental import pallas as pl
from jax.experimental.pallas import tpu as pltpu
from jax.sharding import PartitionSpec as P

MESH = pl.DeviceIdType.MESH
PAD = 8
LANES = 128


def split(x):
    hi = x.astype(jnp.bfloat16)
    lo = (x - hi.astype(jnp.float32)).astype(jnp.bfloat16)
    return hi, lo


def mm(a, b):
    return jnp.dot(a, b, preferred_element_type=jnp.float32)


def mt(a, b):
    return lax.dot_general(
        a, b, (((1,), (1,)), ((), ())), preferred_element_type=jnp.float32
    )


def fold(x):
    out = None
    for y in range(0, x.shape[0], 8):
        for at in range(0, x.shape[1], LANES):
            piece = x[y : y + 8, at : at + LANES]
            out = piece if out is None else out + piece
    return out


def flip(i, mask):
    out, bit = i, 1
    while bit <= mask:
        if mask & bit:
            out = out + bit - 2 * bit * lax.rem(lax.div(i, bit), 2)
        bit *= 2
    return out


def drain(ref, sem):
    pltpu.make_async_copy(ref, ref, sem).wait()


def kernel(
    n, block,
    r_hbm, sg_hbm, wd_hbm, li_hbm, by_hbm, bz_hbm, gm_hbm,
    r, u1, u2, w1, w2, coef,
    sg, wd, wde, lf, by, bz, gm, lh, ll, by3, byt, bzp, bz6, fc,
    sp, sb, sa, ys, yh, yl, hs, hr,
    own, gat, tot, allb, low_s, low_r, nbr, gs, ggat,
    in_sem, as_, ar, bs, br, ls, lr, hss, hsr, gss, gsr, ready, go,
):
    layers, rows, depth = r.shape
    ky = by.shape[0]
    half = ky // 2
    kz = bz.shape[0]
    levels = gm.shape[0]
    blocks = n // block
    low_levels = block.bit_length() - 1
    quarter = rows // 4
    spans = (slice(0, quarter), slice(quarter, rows))
    me = lax.axis_index("sub")
    p = lax.rem(me, block)
    z = lax.div(me, block)
    us = (u1, u2)
    ws = (w1, w2)
    f32 = jnp.float32

    def load(i, src, dst):
        c = pltpu.make_async_copy(src, dst, in_sem.at[i])
        c.start()
        return c

    c_r = load(0, r_hbm, r)
    c_bz = load(1, bz_hbm, bz)
    c_by = load(2, by_hbm, by)
    c_l = load(3, li_hbm, lf)
    c_gm = load(4, gm_hbm, gm)

    barrier = pltpu.get_barrier_semaphore()
    in_block = [z * block + flip(p, d) for d in range(block - 1, 0, -1)]
    across = [lax.rem(z + d, blocks) * block + p for d in range(1, blocks)]
    first_cross = jnp.logical_and(p == 0, z > 0)
    last_cross = jnp.logical_and(p == block - 1, z < blocks - 1)

    late_down = jnp.logical_and(p == block - 2, z > 0)
    late_up = jnp.logical_and(p == 1, z < blocks - 1)

    def signal(target):
        pl.semaphore_signal(barrier, inc=1, device_id=(target,), device_id_type=MESH)

    for target in in_block + across:
        signal(target)

    @pl.when(first_cross)
    def _():
        signal(me - 1)

    @pl.when(last_cross)
    def _():
        signal(me + 1)

    zero_rows = jnp.zeros((PAD, depth), f32)
    for u in us:
        for l in range(layers):
            u[l, 0:PAD, :] = zero_rows
            u[l, PAD + rows : PAD + rows + PAD, :] = zero_rows
    sp[0:PAD, :] = zero_rows
    sp[PAD + rows : PAD + rows + PAD, :] = zero_rows

    @pl.when(me == 0)
    def _():
        hr[:, 0] = jnp.zeros((2, rows, depth), f32)

    @pl.when(me == n - 1)
    def _():
        hr[:, 1] = jnp.zeros((2, rows, depth), f32)

    def send(src, dst, s, q, target):
        return pltpu.make_async_remote_copy(
            src_ref=src, dst_ref=dst, send_sem=s, recv_sem=q,
            device_id=(target,), device_id_type=MESH,
        )

    def project(k):
        hi, lo = yh[...], yl[...]
        bh, bl = bzp[0 : 2 * kz], bzp[2 * kz : 4 * kz]
        part = mt(hi, bh) + mt(lo, bh) + mt(hi, bl)
        ph, pl_ = split(part)
        bh, bl = by3[0:ky], by3[ky : 2 * ky]
        full = mm(bh, ph) + mm(bh, pl_) + mm(bl, ph)
        lane = lax.broadcasted_iota(jnp.int32, (half, 2 * kz), 1)
        packed = jnp.where(lane < kz, full[0:half], full[half:ky])
        own[k] = packed
        gat[k, p] = packed

    def a_send(k):
        for target in in_block:
            send(own.at[k], gat.at[k, p], as_.at[k], ar.at[k], target).start()
        pl.semaphore_signal(
            ready.at[k], inc=1, device_id=(in_block[-1],), device_id_type=MESH
        )

    def a_wait(k, sem):
        drain(gat.at[k, pl.ds(0, block - 1)], sem.at[k])

    def b_send(k):
        for target in across:
            send(tot.at[k], allb.at[k, z], bs.at[k], br.at[k], target).start()

    def b_wait(k, sem):
        if blocks > 1:
            drain(allb.at[k, pl.ds(0, blocks - 1)], sem.at[k])

    def piece(ref, k, way, c):
        at = spans[c]
        return ref.at[k, way, pl.ds(at.start, at.stop - at.start)]

    def down(k, c):
        return send(
            piece(hs, k, 0, c), piece(hr, k, 1, c), hss.at[k, 0], hsr.at[k, 1, c], me - 1
        )

    def up(k, c):
        return send(
            piece(hs, k, 1, c), piece(hr, k, 0, c), hss.at[k, 1], hsr.at[k, 0, c], me + 1
        )

    def low_down(k):
        return send(low_s.at[k, 0], low_r.at[k, 1], ls.at[k, 0], lr.at[k, 1], me - block)

    def low_up(k):
        return send(low_s.at[k, 1], low_r.at[k, 0], ls.at[k, 1], lr.at[k, 0], me + block)

    def allow(k, way, target):
        pl.semaphore_signal(
            go.at[k, way], inc=1, device_id=(target,), device_id_type=MESH
        )

    def cross(k):
        @pl.when(first_cross)
        def _():
            pl.semaphore_wait(go.at[k, 0], 1)
            for c in range(2):
                down(k, c).start()

        @pl.when(last_cross)
        def _():
            pl.semaphore_wait(go.at[k, 1], 1)
            for c in range(2):
                up(k, c).start()

    def later(k):
        @pl.when(late_down)
        def _():
            down(k, 1).start()

        @pl.when(late_up)
        def _():
            up(k, 1).start()

    def edges(k, field):
        u = us[k]
        xh, xl = split(jnp.concatenate([field[0], field[layers - 1]], axis=0))
        out = mm(xh, lh[...]) + mm(xl, lh[...]) + mm(xh, ll[...])
        first, last = out[0:rows], out[rows : 2 * rows]
        hs[k, 0] = first
        hs[k, 1] = last
        u[0, PAD : PAD + rows] = first
        u[layers - 1, PAD : PAD + rows] = last

    def greet(k):
        pl.semaphore_wait(ready.at[k], 1)

        @pl.when(jnp.logical_and(p == block - 1, z > 0))
        def _():
            allow(k, 1, me - block)

        @pl.when(jnp.logical_and(p == 0, z < blocks - 1))
        def _():
            allow(k, 0, me + block)

    def issue(k, c):
        downs, ups = p > 0, p < block - 1
        if c == 1:
            downs = jnp.logical_and(downs, jnp.logical_not(late_down))
            ups = jnp.logical_and(ups, jnp.logical_not(late_up))

        @pl.when(downs)
        def _():
            down(k, c).start()

        @pl.when(ups)
        def _():
            up(k, c).start()

    def middle(k, field):
        u = us[k]
        inner = range(1, layers - 1)
        xh, xl = split(jnp.concatenate([field[l] for l in inner], axis=0))
        out = mm(xh, lh[...]) + mm(xl, lh[...]) + mm(xh, ll[...])
        for i, l in enumerate(inner):
            u[l, PAD : PAD + rows, :] = out[i * rows : (i + 1) * rows]

    def low_part(k, q):
        out = None
        for level in range(low_levels):
            width = 2 ** (level + 1)
            start = lax.div(q, width) * width
            if width == block:
                acc = tot[k]
            else:
                acc = gat[k, start]
                for j in range(1, width):
                    acc = acc + gat[k, start + j]
            term = fc[level] * acc
            out = term if out is None else out + term
        return out

    def high_part(k, zz):
        out = None
        for level in range(low_levels, levels):
            width = 2 ** (level + 1) // block
            start = lax.div(zz, width) * width
            acc = allb[k, start]
            for j in range(1, width):
                acc = acc + allb[k, start + j]
            term = fc[level] * acc
            out = term if out is None else out + term
        return jnp.zeros(tot.shape[1:], f32) if out is None else out

    def exchange(k):
        a_wait(k, ar)
        acc = gat[k, 0]
        for j in range(1, block):
            acc = acc + gat[k, j]
        tot[k] = acc
        allb[k, z] = acc
        b_send(k)

        @pl.when(jnp.logical_and(p == block - 1, z > 0))
        def _():
            low_s[k, 0] = low_part(k, 0)
            low_down(k).start()

        @pl.when(jnp.logical_and(p == 0, z < blocks - 1))
        def _():
            low_s[k, 1] = low_part(k, block - 1)
            low_up(k).start()

        nbr[0] = low_part(k, jnp.maximum(p - 1, 0))
        nbr[1] = low_part(k, p)
        nbr[2] = low_part(k, jnp.minimum(p + 1, block - 1))

        @pl.when(first_cross)
        def _():
            low_up(k).wait_recv()
            nbr[0] = low_r[k, 0]

        @pl.when(last_cross)
        def _():
            low_down(k).wait_recv()
            nbr[2] = low_r[k, 1]

    def back(k):
        b_wait(k, br)
        here = nbr[1] + high_part(k, z)
        before = nbr[0] + high_part(k, lax.div(jnp.maximum(me - 1, 0), block))
        after = nbr[2] + high_part(k, lax.div(jnp.minimum(me + 1, n - 1), block))
        before = jnp.where(me > 0, before, 0.0)
        after = jnp.where(me < n - 1, after, 0.0)
        lane = lax.broadcasted_iota(jnp.int32, (half, 2 * kz), 1)
        three = []
        for c in (here, before, after):
            three += [jnp.where(lane < kz, c, 0.0), jnp.where(lane < kz, 0.0, c)]
        th, tl = split(jnp.concatenate(three, axis=0))
        out = mm(jnp.concatenate([th, tl, th], axis=1), bz6[...])
        th, tl = split(out)
        spreads = []
        for j in range(3):
            piece = slice(j * ky, (j + 1) * ky)
            spreads.append(
                mm(byt[...], jnp.concatenate([th[piece], tl[piece], th[piece]], axis=0))
            )
        sp[PAD : PAD + rows, :] = spreads[0]
        sb[...] = spreads[1]
        sa[...] = spreads[2]

    step = 32

    def beside(ref, l, y):
        a = PAD + y
        here = (lambda s: ref[s, :]) if l is None else (lambda s: ref[l, s, :])
        c = here(slice(a, a + step))
        col = lax.broadcasted_iota(jnp.int32, (step, depth), 1)
        fwd = jnp.where(col == depth - 1, 0.0, pltpu.roll(c, depth - 1, 1))
        bwd = jnp.where(col == 0, 0.0, pltpu.roll(c, 1, 1))
        ups = here(slice(a + 1, a + step + 1))
        downs = here(slice(a - 1, a + step - 1))
        return c, ups + downs + fwd + bwd

    def inner_image(k, which):
        u = us[k]
        for l in which:
            for y in range(0, rows, step):
                a = PAD + y
                at = slice(y, y + step)
                c, around = beside(u, l, y)
                diag = sg[l, at, :] + (4.0 if k == 0 else 0.0)
                out = (2.0 + diag) * c - around
                if k == 0:
                    sg[l, at, :] = diag
                wind = wd[l, at, :]
                if l < layers - 1:
                    out = out + (wind - 1.0) * u[l + 1, a : a + step, :]
                if l > 0:
                    out = out - (wind + 1.0) * u[l - 1, a : a + step, :]
                if k == 0 and l == 0:
                    wde[0, at, :] = wind + 1.0
                if k == 0 and l == layers - 1:
                    wde[1, at, :] = wind - 1.0
                ws[k][l, at, :] = out

    def tally(totals, l, at, out):
        for i, other in enumerate((r, w1, None)):
            other = out if other is None else other[l, at, :]
            term = fold(other * out)
            totals[i] = term if totals[i] is None else totals[i] + term

    outer = (0,) if layers == 1 else (0, layers - 1)

    def image(k, totals):
        w = ws[k]
        for y in range(0, rows, step):
            at = slice(y, y + step)
            s, around = beside(sp, None, y)
            total = None
            for l in range(layers):
                out = w[l, at, :] + (sg[l, at, :] * s - around)
                if l == 0:
                    out = out + wde[0, at, :] * (s - sb[at, :])
                if l == layers - 1:
                    out = out + wde[1, at, :] * (sa[at, :] - s)
                w[l, at, :] = out
                total = out if total is None else total + out
                if k == 1 and l not in outer:
                    tally(totals, l, at, out)
            if k == 0:
                ys[at, :] = total

    def meet(k, c, totals):
        w = ws[k]

        @pl.when(me > 0)
        def _():
            up(k, c).wait_recv()

        @pl.when(me < n - 1)
        def _():
            down(k, c).wait_recv()

        for y in range(spans[c].start, spans[c].stop, quarter):
            at = slice(y, y + quarter)
            change = (-(wde[0, at, :] * hr[k, 0, at, :]), wde[1, at, :] * hr[k, 1, at, :])
            if layers == 1:
                change = (change[0] + change[1],)
            for l, more in zip(outer, change):
                out = w[l, at, :] + more
                w[l, at, :] = out
                if k == 1:
                    tally(totals, l, at, out)
            if k == 0:
                total = ys[at, :]
                for more in change:
                    total = total + more
                yh[at, :], yl[at, :] = split(total)

    def place(totals, first):
        lane = lax.broadcasted_iota(jnp.int32, (8, LANES), 1)
        out = jnp.zeros((8, LANES), f32)
        for i, t in enumerate(totals):
            out = jnp.where(lane == first + i, jnp.sum(t, axis=1, keepdims=True), out)
        return out

    def dots(pairs):
        out = []
        for a, b in pairs:
            acc = None
            for l in range(layers):
                term = fold(a[l] * b[l])
                acc = term if acc is None else acc + term
            out.append(acc)
        return out

    def add_spread(k):
        u = us[k]
        for y in range(0, rows, step):
            s = sp[PAD + y : PAD + y + step, :]
            for l in range(layers):
                u[l, PAD + y : PAD + y + step, :] = u[l, PAD + y : PAD + y + step, :] + s

    c_bz.wait()
    hi, lo = split(bz[...])
    for j in range(2):
        bzp[j * kz : (j + 1) * kz] = hi
        bzp[(2 + j) * kz : (3 + j) * kz] = lo
    for j in range(4):
        bz6[j * kz : (j + 1) * kz] = hi
    for j in range(4, 6):
        bz6[j * kz : (j + 1) * kz] = lo
    c_by.wait()
    hi, lo = split(by[...])
    by3[0:ky] = hi
    by3[ky : 2 * ky] = lo
    c_r.wait()
    for y in range(0, rows, step):
        at = slice(y, y + step)
        total = r[0, at, :]
        for l in range(1, layers):
            total = total + r[l, at, :]
        yh[at, :], yl[at, :] = split(total)
    project(0)
    extra = jnp.where(first_cross, 1, 0) + jnp.where(last_cross, 1, 0)
    pl.semaphore_wait(barrier, block - 1 + blocks - 1 + extra)
    a_send(0)
    c_l.wait()
    c_sg = load(5, sg_hbm, sg)
    c_wd = load(6, wd_hbm, wd)
    big, small = split(lf[0])
    lh[...] = big
    ll[...] = small
    edges(0, r)
    greet(0)
    issue(0, 0)
    issue(0, 1)
    cross(0)
    middle(0, r)
    c_gm.wait()
    for level in range(levels):
        g = gm[level]
        fc[level] = jnp.concatenate([g[0:half], g[half:ky]], axis=1) * (
            (layers * 2 ** (level + 1)) ** -0.5
        )
    hi, lo = split(by[...].T)
    byt[...] = jnp.concatenate([hi, hi, lo], axis=1)
    c_sg.wait()
    c_wd.wait()
    inner_image(0, range(1))
    later(0)
    inner_image(0, range(1, layers))
    exchange(0)
    back(0)
    image(0, None)
    meet(0, 0, None)
    meet(0, 1, None)
    project(1)
    a_send(1)
    edges(1, w1)
    greet(1)
    issue(1, 0)
    issue(1, 1)
    cross(1)
    middle(1, w1)
    add_spread(0)
    inner_image(1, range(1))
    later(1)
    inner_image(1, range(1, layers))
    early = place(dots([(r, r), (r, w1), (w1, w1)]), 0)
    exchange(1)
    back(1)
    totals = [None] * 3
    image(1, totals)
    meet(1, 0, totals)
    meet(1, 1, totals)
    late = place(totals, 3)
    flat = jnp.sum(early + late, axis=0, keepdims=True)
    gs[...] = flat
    ggat[me] = flat
    for d in range(n - 1, 0, -1):
        send(gs, ggat.at[me], gss, gsr, flip(me, d)).start()

    add_spread(1)
    for k in range(2):
        a_wait(k, as_)
        b_wait(k, bs)

        @pl.when(jnp.logical_and(p == block - 1, z > 0))
        def _():
            low_down(k).wait_send()

        @pl.when(jnp.logical_and(p == 0, z < blocks - 1))
        def _():
            low_up(k).wait_send()

        @pl.when(me > 0)
        def _():
            drain(hs.at[k, 0], hss.at[k, 0])

        @pl.when(me < n - 1)
        def _():
            drain(hs.at[k, 1], hss.at[k, 1])

    drain(ggat.at[pl.ds(0, n - 1)], gss)
    drain(ggat.at[pl.ds(0, n - 1)], gsr)
    total = jnp.sum(ggat[...], axis=0)
    g01, g11, g02, g12, g22 = (
        jnp.broadcast_to(total[:, j : j + 1], (1, LANES)) for j in range(1, 6)
    )
    ratio = g12 / g11
    c2 = (g02 - ratio * g01) / (g22 - ratio * g12)
    c1 = g01 / g11 - ratio * c2
    coef[0] = jnp.broadcast_to(c1, (8, LANES))
    coef[1] = jnp.broadcast_to(c2, (8, LANES))


def finish(r, u1, u2, w1, w2, coef, x_hbm, res_hbm, xo, ro, x_sem, res_sem):
    layers, rows, depth = r.shape
    step = 8
    c1 = jnp.concatenate([coef[0]] * (depth // LANES), axis=1)
    c2 = jnp.concatenate([coef[1]] * (depth // LANES), axis=1)
    for l in range(layers):
        for y in range(0, rows, step):
            a = PAD + y
            xo[l, y : y + step, :] = (
                c1 * u1[l, a : a + step, :] + c2 * u2[l, a : a + step, :]
            )
        pltpu.make_async_copy(xo.at[l], x_hbm.at[l], x_sem).start()
    for l in range(layers):
        for y in range(0, rows, step):
            ro[l, y : y + step, :] = (
                r[l, y : y + step, :]
                - c1 * w1[l, y : y + step, :] - c2 * w2[l, y : y + step, :]
            )
        pltpu.make_async_copy(ro.at[l], res_hbm.at[l], res_sem).start()
    drain(xo, x_sem)
    drain(ro, res_sem)


def on_device(right_side, sigma, wind, local_inverse, basis_y, basis_z, gamma):
    n = lax.axis_size("sub")
    block = min(8, n)
    blocks = n // block
    layers, rows, depth = right_side.shape
    ky = basis_y.shape[1]
    kz = basis_z.shape[1]
    f32, bf16 = jnp.float32, jnp.bfloat16
    packed = (ky // 2, 2 * kz)
    cube = pltpu.VMEM((layers, rows, depth), f32)
    padded = pltpu.VMEM((layers, rows + 2 * PAD, depth), f32)
    plane = pltpu.VMEM((rows, depth), f32)
    halo = pltpu.VMEM((2, 2, rows, depth), f32)
    dma = pltpu.SemaphoreType.DMA
    scratch = [
        cube, cube,
        pltpu.VMEM((2, rows, depth), f32),
        pltpu.VMEM((1, depth, depth), f32),
        pltpu.VMEM((ky, rows), f32),
        pltpu.VMEM((kz, depth), f32),
        pltpu.VMEM(gamma.shape, f32),
        pltpu.VMEM((depth, depth), bf16),
        pltpu.VMEM((depth, depth), bf16),
        pltpu.VMEM((2 * ky, rows), bf16),
        pltpu.VMEM((rows, 3 * ky), bf16),
        pltpu.VMEM((4 * kz, depth), bf16),
        pltpu.VMEM((6 * kz, depth), bf16),
        pltpu.VMEM((gamma.shape[0],) + packed, f32),
        pltpu.VMEM((rows + 2 * PAD, depth), f32),
        plane, plane, plane,
        pltpu.VMEM((rows, depth), bf16),
        pltpu.VMEM((rows, depth), bf16),
        halo, halo,
        pltpu.VMEM((2,) + packed, f32),
        pltpu.VMEM((2, block) + packed, f32),
        pltpu.VMEM((2,) + packed, f32),
        pltpu.VMEM((2, blocks) + packed, f32),
        pltpu.VMEM((2, 2) + packed, f32),
        pltpu.VMEM((2, 2) + packed, f32),
        pltpu.VMEM((3,) + packed, f32),
        pltpu.VMEM((1, LANES), f32),
        pltpu.VMEM((n, 1, LANES), f32),
        dma((7,)),
        dma((2,)), dma((2,)),
        dma((2,)), dma((2,)),
        dma((2, 2)), dma((2, 2)),
        dma((2, 2)), dma((2, 2, 2)),
        dma, dma,
        pltpu.SemaphoreType.REGULAR((2,)),
        pltpu.SemaphoreType.REGULAR((2, 2)),
    ]
    hbm = pl.BlockSpec(memory_space=pltpu.HBM)
    vmem = pl.BlockSpec(memory_space=pltpu.VMEM)
    out = jax.ShapeDtypeStruct(right_side.shape, f32)
    pieces = pl.pallas_call(
        functools.partial(kernel, n, block),
        out_shape=(cube, padded, padded, cube, cube, pltpu.VMEM((2, 8, LANES), f32)),
        in_specs=[hbm] * 7,
        out_specs=(vmem,) * 6,
        scratch_shapes=scratch,
        compiler_params=pltpu.CompilerParams(
            collective_id=0, has_side_effects=True, vmem_limit_bytes=50 * 2**20,
        ),
        name="gmres",
    )(right_side, sigma, wind, local_inverse, basis_y.T, basis_z.T, gamma)
    return pl.pallas_call(
        finish,
        out_shape=(out, out),
        in_specs=[vmem] * 6,
        out_specs=(hbm, hbm),
        scratch_shapes=[cube, cube, dma, dma],
        compiler_params=pltpu.CompilerParams(vmem_limit_bytes=24 * 2**20),
        name="finish",
    )(*pieces)


def solution(mesh):
    placed = (
        P("sub", None, None),
        P("sub", None, None),
        P("sub", None, None),
        P("sub", None, None),
        P(),
        P(),
        P(),
    )
    return jax.shard_map(
        on_device,
        mesh=mesh,
        in_specs=placed,
        out_specs=(P("sub", None, None), P("sub", None, None)),
        check_vma=False,
    )
```

time: 32.7 us -> 30.6 us (0.936)
  Pallas kernels: 31.9 us -> 29.8 us
    pallas_call x1, Pallas kernels: 30.5 us -> 28.5 us  [on_device(): pl.pallas_call(functools.partial(kernel, n, block), out_shape=(cube, padd...]
where the time goes in v2:
time: 30.6 us; the launch traced here: 30.5 us
  Pallas kernels  29.8 us (97%)
  between operations  0.64 us (2%)
    pallas_call x1, Pallas kernels, on_device(): pl.pallas_call(functools.partial(kernel, n, block), out_shape=(cube, padd...  28.5 us
    pallas_call x1, Pallas kernels, on_device(): pl.pallas_call(finish, out_shape=(out, out), in_specs=[vmem] * 6, out_spe...  1.35 us

profile of v2, /device:TPU:0, one launch (start us, length us, event | category | flops | bytes accessed | tf_op | source)
XLA Modules:
  0.0 30.5 jit_solution(3643231956165524764)
XLA Ops:
  0.6 28.5 %gmres.1 = (f32[4,128,512]{2,1,0:T(8,128)S(1)}, f32[4,144,512]{2,1,0:T(8,128)S(1)}, f32[4,144,512]{2,1,0:T(8,128)S(1)}, f32[4,128,512]{2,1,0:T(8,128)S(1)}, f32[...) custom-call(f32[4,128,512]{2,1,0:T(8,128)} %r_hbm.1, f32[4,128,512]{2,1,0:T(8,128)} %sg_hbm.1, f32[4,128,512]{2,1,0:T(8,128)} %wd_hbm.1, ...), custom_call_target="tpu_custom_call" | custom-call | tf_op jit(solution)/shard_map/gmres/pallas_call | solution.py:642
  29.1 1.4 %finish.1 = (f32[4,128,512]{2,1,0:T(8,128)}, f32[4,128,512]{2,1,0:T(8,128)}) custom-call(f32[4,128,512]{2,1,0:T(8,128)S(1)} %get-tuple-element.8.r, f32[4,144,512]{2,1,0:T(8,128)S(1)} %get-tuple-element.9.u1, f32[4,144,512]{2,1,0:T(8,128)S(1)} %get-tuple-element.10.u2, f32[4,128,512]{2,1,0:T(8,128)S(1)} %get-tuple-element.11.w1, ...), custom_call_target="tpu_custom_call" | custom-call | tf_op jit(solution)/shard_map/finish/pallas_call | solution.py:653

commit v3 on v2

--- a/solution.py
+++ b/solution.py
@@ -66,7 +66,7 @@
     levels = gm.shape[0]
     blocks = n // block
     low_levels = block.bit_length() - 1
-    quarter = rows // 4
+    quarter = rows // 8
     spans = (slice(0, quarter), slice(quarter, rows))
     me = lax.axis_index("sub")
     p = lax.rem(me, block)
@@ -89,6 +89,12 @@
     barrier = pltpu.get_barrier_semaphore()
     in_block = [z * block + flip(p, d) for d in range(block - 1, 0, -1)]
     across = [lax.rem(z + d, blocks) * block + p for d in range(1, blocks)]
+    beyond = [lax.rem(z + d, blocks) * block + flip(p, 1) for d in range(1, blocks)]
+    odd = lax.rem(p, 2) == 1
+    even = jnp.logical_not(odd)
+    way = lax.rem(p, 2)
+    far, near = way * (layers - 1), (1 - way) * (layers - 1)
+    speaks = jnp.logical_or(jnp.logical_and(odd, p < block - 1), p == block - 2)
     first_cross = jnp.logical_and(p == 0, z > 0)
     last_cross = jnp.logical_and(p == block - 1, z < blocks - 1)
 
@@ -98,7 +104,7 @@
     def signal(target):
         pl.semaphore_signal(barrier, inc=1, device_id=(target,), device_id_type=MESH)
 
-    for target in in_block + across:
+    for target in in_block + across + beyond:
         signal(target)
 
     @pl.when(first_cross)
@@ -133,11 +139,12 @@
 
     def project(k):
         hi, lo = yh[...], yl[...]
+        top = mm(by3[...], hi)
+        part = top[0:ky] + top[ky : 2 * ky] + mm(by3[0:ky], lo)
+        ph, pl_ = split(part)
         bh, bl = bzp[0 : 2 * kz], bzp[2 * kz : 4 * kz]
-        part = mt(hi, bh) + mt(lo, bh) + mt(hi, bl)
-        ph, pl_ = split(part)
-        bh, bl = by3[0:ky], by3[ky : 2 * ky]
-        full = mm(bh, ph) + mm(bh, pl_) + mm(bl, ph)
+        top = mt(jnp.concatenate([ph, pl_], axis=0), bh)
+        full = top[0:ky] + top[ky : 2 * ky] + mt(ph, bl)
         lane = lax.broadcasted_iota(jnp.int32, (half, 2 * kz), 1)
         packed = jnp.where(lane < kz, full[0:half], full[half:ky])
         own[k] = packed
@@ -154,8 +161,10 @@
         drain(gat.at[k, pl.ds(0, block - 1)], sem.at[k])
 
     def b_send(k):
-        for target in across:
-            send(tot.at[k], allb.at[k, z], bs.at[k], br.at[k], target).start()
+        @pl.when(speaks)
+        def _():
+            for target in across + beyond:
+                send(tot.at[k], allb.at[k, z], bs.at[k], br.at[k], target).start()
 
     def b_wait(k, sem):
         if blocks > 1:
@@ -208,15 +217,24 @@
         def _():
             up(k, 1).start()
 
-    def edges(k, field):
-        u = us[k]
-        xh, xl = split(jnp.concatenate([field[0], field[layers - 1]], axis=0))
-        out = mm(xh, lh[...]) + mm(xl, lh[...]) + mm(xh, ll[...])
-        first, last = out[0:rows], out[rows : 2 * rows]
-        hs[k, 0] = first
-        hs[k, 1] = last
-        u[0, PAD : PAD + rows] = first
-        u[layers - 1, PAD : PAD + rows] = last
+    def times(x):
+        xh, xl = split(x)
+        m = x.shape[0]
+        both = mm(jnp.concatenate([xh, xl], axis=0), lh[...])
+        return both[0:m] + both[m : 2 * m] + mm(xh, ll[...])
+
+    def far_edge(k, field, at):
+        out = times(field[far, at])
+        hs[k, way, at] = out
+        us[k][far, PAD + at.start : PAD + at.stop] = out
+
+    def others(k, field):
+        inner = range(1, layers - 1)
+        out = times(jnp.concatenate([field[near]] + [field[l] for l in inner], axis=0))
+        hs[k, 1 - way] = out[0:rows]
+        us[k][near, PAD : PAD + rows] = out[0:rows]
+        for i, l in enumerate(inner):
+            us[k][l, PAD : PAD + rows, :] = out[(i + 1) * rows : (i + 2) * rows]
 
     def greet(k):
         pl.semaphore_wait(ready.at[k], 1)
@@ -230,7 +248,7 @@
             allow(k, 0, me + block)
 
     def issue(k, c):
-        downs, ups = p > 0, p < block - 1
+        downs, ups = jnp.logical_and(even, p > 0), jnp.logical_and(odd, p < block - 1)
         if c == 1:
             downs = jnp.logical_and(downs, jnp.logical_not(late_down))
             ups = jnp.logical_and(ups, jnp.logical_not(late_up))
@@ -243,13 +261,16 @@
         def _():
             up(k, c).start()
 
-    def middle(k, field):
-        u = us[k]
-        inner = range(1, layers - 1)
-        xh, xl = split(jnp.concatenate([field[l] for l in inner], axis=0))
-        out = mm(xh, lh[...]) + mm(xl, lh[...]) + mm(xh, ll[...])
-        for i, l in enumerate(inner):
-            u[l, PAD : PAD + rows, :] = out[i * rows : (i + 1) * rows]
+    def issue_near(k):
+        @pl.when(even)
+        def _():
+            for c in range(2):
+                up(k, c).start()
+
+        @pl.when(odd)
+        def _():
+            for c in range(2):
+                down(k, c).start()
 
     def low_part(k, q):
         out = None
@@ -470,7 +491,7 @@
         yh[at, :], yl[at, :] = split(total)
     project(0)
     extra = jnp.where(first_cross, 1, 0) + jnp.where(last_cross, 1, 0)
-    pl.semaphore_wait(barrier, block - 1 + blocks - 1 + extra)
+    pl.semaphore_wait(barrier, block - 1 + 2 * (blocks - 1) + extra)
     a_send(0)
     c_l.wait()
     c_sg = load(5, sg_hbm, sg)
@@ -478,12 +499,13 @@
     big, small = split(lf[0])
     lh[...] = big
     ll[...] = small
-    edges(0, r)
+    far_edge(0, r, slice(0, rows))
     greet(0)
     issue(0, 0)
     issue(0, 1)
     cross(0)
-    middle(0, r)
+    others(0, r)
+    issue_near(0)
     c_gm.wait()
     for level in range(levels):
         g = gm[level]
@@ -501,15 +523,17 @@
     back(0)
     image(0, None)
     meet(0, 0, None)
+    far_edge(1, w1, spans[0])
+    issue(1, 0)
     meet(0, 1, None)
     project(1)
     a_send(1)
-    edges(1, w1)
+    far_edge(1, w1, spans[1])
     greet(1)
-    issue(1, 0)
     issue(1, 1)
     cross(1)
-    middle(1, w1)
+    others(1, w1)
+    issue_near(1)
     add_spread(0)
     inner_image(1, range(1))
     later(1)
@@ -531,7 +555,11 @@
     add_spread(1)
     for k in range(2):
         a_wait(k, as_)
-        b_wait(k, bs)
+
+        @pl.when(speaks)
+        def _():
+            b_wait(k, bs)
+            b_wait(k, bs)
 
         @pl.when(jnp.logical_and(p == block - 1, z > 0))
         def _():

time: 30.6 us -> 29.6 us (0.967)
  Pallas kernels: 29.8 us -> 28.8 us
    pallas_call x1, Pallas kernels: 28.5 us -> 27.4 us  [on_device(): pl.pallas_call(functools.partial(kernel, n, block), out_shape=(cube, padd...]
where the time goes in v3:
time: 29.6 us; the launch traced here: 29.4 us
  Pallas kernels  28.8 us (97%)
  between operations  0.64 us (2%)
    pallas_call x1, Pallas kernels, on_device(): pl.pallas_call(functools.partial(kernel, n, block), out_shape=(cube, padd...  27.4 us
    pallas_call x1, Pallas kernels, on_device(): pl.pallas_call(finish, out_shape=(out, out), in_specs=[vmem] * 6, out_spe...  1.35 us

profile of v3, /device:TPU:0, one launch (start us, length us, event | category | flops | bytes accessed | tf_op | source)
XLA Modules:
  0.0 29.4 jit_solution(3269892183026095309)
XLA Ops:
  0.6 27.4 %gmres.1 = (f32[4,128,512]{2,1,0:T(8,128)S(1)}, f32[4,144,512]{2,1,0:T(8,128)S(1)}, f32[4,144,512]{2,1,0:T(8,128)S(1)}, f32[4,128,512]{2,1,0:T(8,128)S(1)}, f32[...) custom-call(f32[4,128,512]{2,1,0:T(8,128)} %r_hbm.1, f32[4,128,512]{2,1,0:T(8,128)} %sg_hbm.1, f32[4,128,512]{2,1,0:T(8,128)} %wd_hbm.1, ...), custom_call_target="tpu_custom_call" | custom-call | tf_op jit(solution)/shard_map/gmres/pallas_call | solution.py:670
  28.0 1.4 %finish.1 = (f32[4,128,512]{2,1,0:T(8,128)}, f32[4,128,512]{2,1,0:T(8,128)}) custom-call(f32[4,128,512]{2,1,0:T(8,128)S(1)} %get-tuple-element.8.r, f32[4,144,512]{2,1,0:T(8,128)S(1)} %get-tuple-element.9.u1, f32[4,144,512]{2,1,0:T(8,128)S(1)} %get-tuple-element.10.u2, f32[4,128,512]{2,1,0:T(8,128)S(1)} %get-tuple-element.11.w1, ...), custom_call_target="tpu_custom_call" | custom-call | tf_op jit(solution)/shard_map/finish/pallas_call | solution.py:681

commit v4 on v3

--- a/solution.py
+++ b/solution.py
@@ -54,7 +54,7 @@
     n, block,
     r_hbm, sg_hbm, wd_hbm, li_hbm, by_hbm, bz_hbm, gm_hbm,
     r, u1, u2, w1, w2, coef,
-    sg, wd, wde, lf, by, bz, gm, lh, ll, by3, byt, bzp, bz6, fc,
+    sw, wde, lf, by, bz, gm, lh, ll, by3, byt, bzp, bz6, fc,
     sp, sb, sa, ys, yh, yl, hs, hr,
     own, gat, tot, allb, low_s, low_r, nbr, gs, ggat,
     in_sem, as_, ar, bs, br, ls, lr, hss, hsr, gss, gsr, ready, go,
@@ -68,10 +68,12 @@
     low_levels = block.bit_length() - 1
     quarter = rows // 8
     spans = (slice(0, quarter), slice(quarter, rows))
+    cuts = (0, quarter, 3 * quarter, rows * 11 // 16, rows)
     me = lax.axis_index("sub")
     p = lax.rem(me, block)
     z = lax.div(me, block)
     us = (u1, u2)
+    sg, wd = sw.at[0], sw.at[1]
     ws = (w1, w2)
     f32 = jnp.float32
 
@@ -80,9 +82,9 @@
         c.start()
         return c
 
-    c_r = load(0, r_hbm, r)
     c_bz = load(1, bz_hbm, bz)
     c_by = load(2, by_hbm, by)
+    c_r = load(0, r_hbm, r)
     c_l = load(3, li_hbm, lf)
     c_gm = load(4, gm_hbm, gm)
 
@@ -98,8 +100,6 @@
     first_cross = jnp.logical_and(p == 0, z > 0)
     last_cross = jnp.logical_and(p == block - 1, z < blocks - 1)
 
-    late_down = jnp.logical_and(p == block - 2, z > 0)
-    late_up = jnp.logical_and(p == 1, z < blocks - 1)
 
     def signal(target):
         pl.semaphore_signal(barrier, inc=1, device_id=(target,), device_id_type=MESH)
@@ -170,52 +170,47 @@
         if blocks > 1:
             drain(allb.at[k, pl.ds(0, blocks - 1)], sem.at[k])
 
-    def piece(ref, k, way, c):
-        at = spans[c]
+    def piece(ref, k, way, at):
         return ref.at[k, way, pl.ds(at.start, at.stop - at.start)]
 
-    def down(k, c):
+    def down(k, c, at):
         return send(
-            piece(hs, k, 0, c), piece(hr, k, 1, c), hss.at[k, 0], hsr.at[k, 1, c], me - 1
+            piece(hs, k, 0, at), piece(hr, k, 1, at), hss.at[k, 0], hsr.at[k, 1, c], me - 1
         )
 
-    def up(k, c):
+    def up(k, c, at):
         return send(
-            piece(hs, k, 1, c), piece(hr, k, 0, c), hss.at[k, 1], hsr.at[k, 0, c], me + 1
+            piece(hs, k, 1, at), piece(hr, k, 0, at), hss.at[k, 1], hsr.at[k, 0, c], me + 1
         )
 
     def low_down(k):
-        return send(low_s.at[k, 0], low_r.at[k, 1], ls.at[k, 0], lr.at[k, 1], me - block)
+        return send(low_s.at[k, 0], low_r.at[k, 1], ls.at[k], lr.at[k], me - block)
 
     def low_up(k):
-        return send(low_s.at[k, 1], low_r.at[k, 0], ls.at[k, 1], lr.at[k, 0], me + block)
-
-    def allow(k, way, target):
+        return send(low_s.at[k, 1], low_r.at[k, 0], ls.at[k], lr.at[k], me + block)
+
+    def allow(k, target):
         pl.semaphore_signal(
-            go.at[k, way], inc=1, device_id=(target,), device_id_type=MESH
+            go.at[k], inc=1, device_id=(target,), device_id_type=MESH
         )
 
-    def cross(k):
+    def part(i):
+        return min(i, 1), slice(cuts[i], cuts[i + 1])
+
+    def cross(k, which):
         @pl.when(first_cross)
         def _():
-            pl.semaphore_wait(go.at[k, 0], 1)
-            for c in range(2):
-                down(k, c).start()
+            if 0 in which:
+                pl.semaphore_wait(go.at[k], 1)
+            for i in which:
+                down(k, *part(i)).start()
 
         @pl.when(last_cross)
         def _():
-            pl.semaphore_wait(go.at[k, 1], 1)
-            for c in range(2):
-                up(k, c).start()
-
-    def later(k):
-        @pl.when(late_down)
-        def _():
-            down(k, 1).start()
-
-        @pl.when(late_up)
-        def _():
-            up(k, 1).start()
+            if 0 in which:
+                pl.semaphore_wait(go.at[k], 1)
+            for i in which:
+                up(k, *part(i)).start()
 
     def times(x):
         xh, xl = split(x)
@@ -241,36 +236,33 @@
 
         @pl.when(jnp.logical_and(p == block - 1, z > 0))
         def _():
-            allow(k, 1, me - block)
+            allow(k, me - block)
 
         @pl.when(jnp.logical_and(p == 0, z < blocks - 1))
         def _():
-            allow(k, 0, me + block)
-
-    def issue(k, c):
-        downs, ups = jnp.logical_and(even, p > 0), jnp.logical_and(odd, p < block - 1)
-        if c == 1:
-            downs = jnp.logical_and(downs, jnp.logical_not(late_down))
-            ups = jnp.logical_and(ups, jnp.logical_not(late_up))
-
-        @pl.when(downs)
-        def _():
-            down(k, c).start()
-
-        @pl.when(ups)
-        def _():
-            up(k, c).start()
+            allow(k, me + block)
+
+    def issue(k, which):
+        @pl.when(jnp.logical_and(even, p > 0))
+        def _():
+            for i in which:
+                down(k, *part(i)).start()
+
+        @pl.when(jnp.logical_and(odd, p < block - 1))
+        def _():
+            for i in which:
+                up(k, *part(i)).start()
 
     def issue_near(k):
         @pl.when(even)
         def _():
             for c in range(2):
-                up(k, c).start()
+                up(k, c, spans[c]).start()
 
         @pl.when(odd)
         def _():
             for c in range(2):
-                down(k, c).start()
+                down(k, c, spans[c]).start()
 
     def low_part(k, q):
         out = None
@@ -423,11 +415,11 @@
 
         @pl.when(me > 0)
         def _():
-            up(k, c).wait_recv()
+            up(k, c, spans[c]).wait_recv()
 
         @pl.when(me < n - 1)
         def _():
-            down(k, c).wait_recv()
+            down(k, c, spans[c]).wait_recv()
 
         for y in range(spans[c].start, spans[c].stop, quarter):
             at = slice(y, y + quarter)
@@ -494,18 +486,19 @@
     pl.semaphore_wait(barrier, block - 1 + 2 * (blocks - 1) + extra)
     a_send(0)
     c_l.wait()
-    c_sg = load(5, sg_hbm, sg)
-    c_wd = load(6, wd_hbm, wd)
+    pltpu.make_async_copy(sg_hbm, sw.at[0], in_sem.at[5]).start()
+    pltpu.make_async_copy(wd_hbm, sw.at[1], in_sem.at[5]).start()
     big, small = split(lf[0])
     lh[...] = big
     ll[...] = small
     far_edge(0, r, slice(0, rows))
     greet(0)
-    issue(0, 0)
-    issue(0, 1)
-    cross(0)
+    issue(0, (0, 1))
+    cross(0, (0, 1))
     others(0, r)
     issue_near(0)
+    issue(0, (2,))
+    cross(0, (2,))
     c_gm.wait()
     for level in range(levels):
         g = gm[level]
@@ -514,29 +507,32 @@
         )
     hi, lo = split(by[...].T)
     byt[...] = jnp.concatenate([hi, hi, lo], axis=1)
-    c_sg.wait()
-    c_wd.wait()
+    drain(sw, in_sem.at[5])
     inner_image(0, range(1))
-    later(0)
+    issue(0, (3,))
+    cross(0, (3,))
     inner_image(0, range(1, layers))
     exchange(0)
     back(0)
     image(0, None)
     meet(0, 0, None)
     far_edge(1, w1, spans[0])
-    issue(1, 0)
+    issue(1, (0,))
     meet(0, 1, None)
     project(1)
     a_send(1)
     far_edge(1, w1, spans[1])
     greet(1)
-    issue(1, 1)
-    cross(1)
+    issue(1, (1,))
+    cross(1, (0, 1))
     others(1, w1)
     issue_near(1)
+    issue(1, (2,))
+    cross(1, (2,))
     add_spread(0)
     inner_image(1, range(1))
-    later(1)
+    issue(1, (3,))
+    cross(1, (3,))
     inner_image(1, range(1, layers))
     early = place(dots([(r, r), (r, w1), (w1, w1)]), 0)
     exchange(1)
@@ -592,23 +588,27 @@
 
 def finish(r, u1, u2, w1, w2, coef, x_hbm, res_hbm, xo, ro, x_sem, res_sem):
     layers, rows, depth = r.shape
-    step = 8
+    step, part = 8, 32
     c1 = jnp.concatenate([coef[0]] * (depth // LANES), axis=1)
     c2 = jnp.concatenate([coef[1]] * (depth // LANES), axis=1)
+
+    def flush(buf, out, l, y, sem):
+        at = pl.ds(y, part)
+        pltpu.make_async_copy(buf.at[l, at], out.at[l, at], sem).start()
+
     for l in range(layers):
         for y in range(0, rows, step):
             a = PAD + y
             xo[l, y : y + step, :] = (
                 c1 * u1[l, a : a + step, :] + c2 * u2[l, a : a + step, :]
             )
-        pltpu.make_async_copy(xo.at[l], x_hbm.at[l], x_sem).start()
-    for l in range(layers):
-        for y in range(0, rows, step):
             ro[l, y : y + step, :] = (
                 r[l, y : y + step, :]
                 - c1 * w1[l, y : y + step, :] - c2 * w2[l, y : y + step, :]
             )
-        pltpu.make_async_copy(ro.at[l], res_hbm.at[l], res_sem).start()
+            if (y + step) % part == 0:
+                flush(xo, x_hbm, l, y + step - part, x_sem)
+                flush(ro, res_hbm, l, y + step - part, res_sem)
     drain(xo, x_sem)
     drain(ro, res_sem)
 
@@ -628,7 +628,7 @@
     halo = pltpu.VMEM((2, 2, rows, depth), f32)
     dma = pltpu.SemaphoreType.DMA
     scratch = [
-        cube, cube,
+        pltpu.VMEM((2, layers, rows, depth), f32),
         pltpu.VMEM((2, rows, depth), f32),
         pltpu.VMEM((1, depth, depth), f32),
         pltpu.VMEM((ky, rows), f32),
@@ -655,14 +655,14 @@
         pltpu.VMEM((3,) + packed, f32),
         pltpu.VMEM((1, LANES), f32),
         pltpu.VMEM((n, 1, LANES), f32),
-        dma((7,)),
+        dma((6,)),
         dma((2,)), dma((2,)),
         dma((2,)), dma((2,)),
-        dma((2, 2)), dma((2, 2)),
+        dma((2,)), dma((2,)),
         dma((2, 2)), dma((2, 2, 2)),
         dma, dma,
         pltpu.SemaphoreType.REGULAR((2,)),
-        pltpu.SemaphoreType.REGULAR((2, 2)),
+        pltpu.SemaphoreType.REGULAR((2,)),
     ]
     hbm = pl.BlockSpec(memory_space=pltpu.HBM)
     vmem = pl.BlockSpec(memory_space=pltpu.VMEM)

time: 29.6 us -> 29.5 us (level)
  no operation moved by 1% of the time
where the time goes in v4:
time: 29.5 us; the launch traced here: 29.3 us
  Pallas kernels  28.7 us (97%)
  between operations  0.64 us (2%)
    pallas_call x1, Pallas kernels, on_device(): pl.pallas_call(functools.partial(kernel, n, block), out_shape=(cube, padd...  27.3 us
    pallas_call x1, Pallas kernels, on_device(): pl.pallas_call(finish, out_shape=(out, out), in_specs=[vmem] * 6, out_spe...  1.32 us

profile of v4, /device:TPU:0, one launch (start us, length us, event | category | flops | bytes accessed | tf_op | source)
XLA Modules:
  0.0 29.3 jit_solution(12141353909565579043)
XLA Ops:
  0.6 27.3 %gmres.1 = (f32[4,128,512]{2,1,0:T(8,128)S(1)}, f32[4,144,512]{2,1,0:T(8,128)S(1)}, f32[4,144,512]{2,1,0:T(8,128)S(1)}, f32[4,128,512]{2,1,0:T(8,128)S(1)}, f32[...) custom-call(f32[4,128,512]{2,1,0:T(8,128)} %r_hbm.1, f32[4,128,512]{2,1,0:T(8,128)} %sg_hbm.1, f32[4,128,512]{2,1,0:T(8,128)} %wd_hbm.1, ...), custom_call_target="tpu_custom_call" | custom-call | tf_op jit(solution)/shard_map/gmres/pallas_call | solution.py:670
  28.0 1.3 %finish.1 = (f32[4,128,512]{2,1,0:T(8,128)}, f32[4,128,512]{2,1,0:T(8,128)}) custom-call(f32[4,128,512]{2,1,0:T(8,128)S(1)} %get-tuple-element.8.r, f32[4,144,512]{2,1,0:T(8,128)S(1)} %get-tuple-element.9.u1, f32[4,144,512]{2,1,0:T(8,128)S(1)} %get-tuple-element.10.u2, f32[4,128,512]{2,1,0:T(8,128)S(1)} %get-tuple-element.11.w1, ...), custom_call_target="tpu_custom_call" | custom-call | tf_op jit(solution)/shard_map/finish/pallas_call | solution.py:681

commit v5 on v4

--- a/solution.py
+++ b/solution.py
@@ -57,7 +57,7 @@
     sw, wde, lf, by, bz, gm, lh, ll, by3, byt, bzp, bz6, fc,
     sp, sb, sa, ys, yh, yl, hs, hr,
     own, gat, tot, allb, low_s, low_r, nbr, gs, ggat,
-    in_sem, as_, ar, bs, br, ls, lr, hss, hsr, gss, gsr, ready, go,
+    in_sem, out_sem, ar, br, lr, hsr, gsr, ready, go,
 ):
     layers, rows, depth = r.shape
     ky = by.shape[0]
@@ -66,9 +66,9 @@
     levels = gm.shape[0]
     blocks = n // block
     low_levels = block.bit_length() - 1
-    quarter = rows // 8
+    quarter = rows // 4
     spans = (slice(0, quarter), slice(quarter, rows))
-    cuts = (0, quarter, 3 * quarter, rows * 11 // 16, rows)
+    cuts = (0, quarter, 2 * quarter, 3 * quarter, rows)
     me = lax.axis_index("sub")
     p = lax.rem(me, block)
     z = lax.div(me, block)
@@ -96,7 +96,7 @@
     even = jnp.logical_not(odd)
     way = lax.rem(p, 2)
     far, near = way * (layers - 1), (1 - way) * (layers - 1)
-    speaks = jnp.logical_or(jnp.logical_and(odd, p < block - 1), p == block - 2)
+    speaks = odd
     first_cross = jnp.logical_and(p == 0, z > 0)
     last_cross = jnp.logical_and(p == block - 1, z < blocks - 1)
 
@@ -152,42 +152,42 @@
 
     def a_send(k):
         for target in in_block:
-            send(own.at[k], gat.at[k, p], as_.at[k], ar.at[k], target).start()
+            send(own.at[k], gat.at[k, p], out_sem, ar.at[k], target).start()
         pl.semaphore_signal(
             ready.at[k], inc=1, device_id=(in_block[-1],), device_id_type=MESH
         )
 
     def a_wait(k, sem):
-        drain(gat.at[k, pl.ds(0, block - 1)], sem.at[k])
+        drain(gat.at[k, pl.ds(0, block - 1)], sem)
 
     def b_send(k):
         @pl.when(speaks)
         def _():
             for target in across + beyond:
-                send(tot.at[k], allb.at[k, z], bs.at[k], br.at[k], target).start()
+                send(tot.at[k], allb.at[k, z], out_sem, br.at[k], target).start()
 
     def b_wait(k, sem):
         if blocks > 1:
-            drain(allb.at[k, pl.ds(0, blocks - 1)], sem.at[k])
+            drain(allb.at[k, pl.ds(0, blocks - 1)], sem)
 
     def piece(ref, k, way, at):
         return ref.at[k, way, pl.ds(at.start, at.stop - at.start)]
 
     def down(k, c, at):
         return send(
-            piece(hs, k, 0, at), piece(hr, k, 1, at), hss.at[k, 0], hsr.at[k, 1, c], me - 1
+            piece(hs, k, 0, at), piece(hr, k, 1, at), out_sem, hsr.at[k, 1, c], me - 1
         )
 
     def up(k, c, at):
         return send(
-            piece(hs, k, 1, at), piece(hr, k, 0, at), hss.at[k, 1], hsr.at[k, 0, c], me + 1
+            piece(hs, k, 1, at), piece(hr, k, 0, at), out_sem, hsr.at[k, 0, c], me + 1
         )
 
     def low_down(k):
-        return send(low_s.at[k, 0], low_r.at[k, 1], ls.at[k], lr.at[k], me - block)
+        return send(low_s.at[k, 0], low_r.at[k, 1], out_sem, lr.at[k], me - block)
 
     def low_up(k):
-        return send(low_s.at[k, 1], low_r.at[k, 0], ls.at[k], lr.at[k], me + block)
+        return send(low_s.at[k, 1], low_r.at[k, 0], out_sem, lr.at[k], me + block)
 
     def allow(k, target):
         pl.semaphore_signal(
@@ -292,7 +292,7 @@
         return jnp.zeros(tot.shape[1:], f32) if out is None else out
 
     def exchange(k):
-        a_wait(k, ar)
+        a_wait(k, ar.at[k])
         acc = gat[k, 0]
         for j in range(1, block):
             acc = acc + gat[k, j]
@@ -325,7 +325,7 @@
             nbr[2] = low_r[k, 1]
 
     def back(k):
-        b_wait(k, br)
+        b_wait(k, br.at[k])
         here = nbr[1] + high_part(k, z)
         before = nbr[0] + high_part(k, lax.div(jnp.maximum(me - 1, 0), block))
         after = nbr[2] + high_part(k, lax.div(jnp.minimum(me + 1, n - 1), block))
@@ -466,10 +466,6 @@
     for j in range(2):
         bzp[j * kz : (j + 1) * kz] = hi
         bzp[(2 + j) * kz : (3 + j) * kz] = lo
-    for j in range(4):
-        bz6[j * kz : (j + 1) * kz] = hi
-    for j in range(4, 6):
-        bz6[j * kz : (j + 1) * kz] = lo
     c_by.wait()
     hi, lo = split(by[...])
     by3[0:ky] = hi
@@ -505,6 +501,9 @@
         fc[level] = jnp.concatenate([g[0:half], g[half:ky]], axis=1) * (
             (layers * 2 ** (level + 1)) ** -0.5
         )
+    for j in range(2):
+        bz6[2 * j * kz : (2 * j + 2) * kz] = bzp[0 : 2 * kz]
+    bz6[4 * kz : 6 * kz] = bzp[2 * kz : 4 * kz]
     hi, lo = split(by[...].T)
     byt[...] = jnp.concatenate([hi, hi, lo], axis=1)
     drain(sw, in_sem.at[5])
@@ -546,16 +545,16 @@
     gs[...] = flat
     ggat[me] = flat
     for d in range(n - 1, 0, -1):
-        send(gs, ggat.at[me], gss, gsr, flip(me, d)).start()
+        send(gs, ggat.at[me], out_sem, gsr, flip(me, d)).start()
 
     add_spread(1)
     for k in range(2):
-        a_wait(k, as_)
+        a_wait(k, out_sem)
 
         @pl.when(speaks)
         def _():
-            b_wait(k, bs)
-            b_wait(k, bs)
+            b_wait(k, out_sem)
+            b_wait(k, out_sem)
 
         @pl.when(jnp.logical_and(p == block - 1, z > 0))
         def _():
@@ -567,13 +566,13 @@
 
         @pl.when(me > 0)
         def _():
-            drain(hs.at[k, 0], hss.at[k, 0])
+            drain(hs.at[k, 0], out_sem)
 
         @pl.when(me < n - 1)
         def _():
-            drain(hs.at[k, 1], hss.at[k, 1])
-
-    drain(ggat.at[pl.ds(0, n - 1)], gss)
+            drain(hs.at[k, 1], out_sem)
+
+    drain(ggat.at[pl.ds(0, n - 1)], out_sem)
     drain(ggat.at[pl.ds(0, n - 1)], gsr)
     total = jnp.sum(ggat[...], axis=0)
     g01, g11, g02, g12, g22 = (
@@ -655,12 +654,9 @@
         pltpu.VMEM((3,) + packed, f32),
         pltpu.VMEM((1, LANES), f32),
         pltpu.VMEM((n, 1, LANES), f32),
-        dma((6,)),
-        dma((2,)), dma((2,)),
-        dma((2,)), dma((2,)),
-        dma((2,)), dma((2,)),
-        dma((2, 2)), dma((2, 2, 2)),
-        dma, dma,
+        dma((6,)), dma,
+        dma((2,)), dma((2,)), dma((2,)), dma((2, 2, 2)),
+        dma,
         pltpu.SemaphoreType.REGULAR((2,)),
         pltpu.SemaphoreType.REGULAR((2,)),
     ]

time: 29.5 us -> 29.2 us (0.990)
  Pallas kernels: 28.7 us -> 28.4 us
where the time goes in v5:
time: 29.2 us; the launch traced here: 29 us
  Pallas kernels  28.4 us (97%)
  between operations  0.64 us (2%)
    pallas_call x1, Pallas kernels, on_device(): pl.pallas_call(functools.partial(kernel, n, block), out_shape=(cube, padd...  27 us
    pallas_call x1, Pallas kernels, on_device(): pl.pallas_call(finish, out_shape=(out, out), in_specs=[vmem] * 6, out_spe...  1.32 us

profile of v5, /device:TPU:0, one launch (start us, length us, event | category | flops | bytes accessed | tf_op | source)
XLA Modules:
  0.0 29.0 jit_solution(7868545739352022757)
XLA Ops:
  0.6 27.0 %gmres.1 = (f32[4,128,512]{2,1,0:T(8,128)S(1)}, f32[4,144,512]{2,1,0:T(8,128)S(1)}, f32[4,144,512]{2,1,0:T(8,128)S(1)}, f32[4,128,512]{2,1,0:T(8,128)S(1)}, f32[...) custom-call(f32[4,128,512]{2,1,0:T(8,128)} %r_hbm.1, f32[4,128,512]{2,1,0:T(8,128)} %sg_hbm.1, f32[4,128,512]{2,1,0:T(8,128)} %wd_hbm.1, ...), custom_call_target="tpu_custom_call" | custom-call | tf_op jit(solution)/shard_map/gmres/pallas_call | solution.py:666
  27.7 1.3 %finish.1 = (f32[4,128,512]{2,1,0:T(8,128)}, f32[4,128,512]{2,1,0:T(8,128)}) custom-call(f32[4,128,512]{2,1,0:T(8,128)S(1)} %get-tuple-element.8.r, f32[4,144,512]{2,1,0:T(8,128)S(1)} %get-tuple-element.9.u1, f32[4,144,512]{2,1,0:T(8,128)S(1)} %get-tuple-element.10.u2, f32[4,128,512]{2,1,0:T(8,128)S(1)} %get-tuple-element.11.w1, ...), custom_call_target="tpu_custom_call" | custom-call | tf_op jit(solution)/shard_map/finish/pallas_call | solution.py:677

commit v6 on v5

--- a/solution.py
+++ b/solution.py
@@ -85,8 +85,6 @@
     c_bz = load(1, bz_hbm, bz)
     c_by = load(2, by_hbm, by)
     c_r = load(0, r_hbm, r)
-    c_l = load(3, li_hbm, lf)
-    c_gm = load(4, gm_hbm, gm)
 
     barrier = pltpu.get_barrier_semaphore()
     in_block = [z * block + flip(p, d) for d in range(block - 1, 0, -1)]
@@ -462,6 +460,8 @@
                 u[l, PAD + y : PAD + y + step, :] = u[l, PAD + y : PAD + y + step, :] + s
 
     c_bz.wait()
+    c_l = load(3, li_hbm, lf)
+    c_gm = load(4, gm_hbm, gm)
     hi, lo = split(bz[...])
     for j in range(2):
         bzp[j * kz : (j + 1) * kz] = hi

time: 29.2 us -> 29.2 us (level)
  no operation moved by 1% of the time
where the time goes in v6:
time: 29.2 us; the launch traced here: 29 us
  Pallas kernels  28.4 us (97%)
  between operations  0.64 us (2%)
    pallas_call x1, Pallas kernels, on_device(): pl.pallas_call(functools.partial(kernel, n, block), out_shape=(cube, padd...  27 us
    pallas_call x1, Pallas kernels, on_device(): pl.pallas_call(finish, out_shape=(out, out), in_specs=[vmem] * 6, out_spe...  1.32 us

profile of v6, /device:TPU:0, one launch (start us, length us, event | category | flops | bytes accessed | tf_op | source)
XLA Modules:
  0.0 29.0 jit_solution(12809343646687615466)
XLA Ops:
  0.6 27.0 %gmres.1 = (f32[4,128,512]{2,1,0:T(8,128)S(1)}, f32[4,144,512]{2,1,0:T(8,128)S(1)}, f32[4,144,512]{2,1,0:T(8,128)S(1)}, f32[4,128,512]{2,1,0:T(8,128)S(1)}, f32[...) custom-call(f32[4,128,512]{2,1,0:T(8,128)} %r_hbm.1, f32[4,128,512]{2,1,0:T(8,128)} %sg_hbm.1, f32[4,128,512]{2,1,0:T(8,128)} %wd_hbm.1, ...), custom_call_target="tpu_custom_call" | custom-call | tf_op jit(solution)/shard_map/gmres/pallas_call | solution.py:666
  27.7 1.3 %finish.1 = (f32[4,128,512]{2,1,0:T(8,128)}, f32[4,128,512]{2,1,0:T(8,128)}) custom-call(f32[4,128,512]{2,1,0:T(8,128)S(1)} %get-tuple-element.8.r, f32[4,144,512]{2,1,0:T(8,128)S(1)} %get-tuple-element.9.u1, f32[4,144,512]{2,1,0:T(8,128)S(1)} %get-tuple-element.10.u2, f32[4,128,512]{2,1,0:T(8,128)S(1)} %get-tuple-element.11.w1, ...), custom_call_target="tpu_custom_call" | custom-call | tf_op jit(solution)/shard_map/finish/pallas_call | solution.py:677
